TPU v7x, 32 devices: a whole 2x2x4 slice. The times are simulated.
32 devices in a mesh: dp: 8 (over y, x, core), mp: 4 (over z).
Axes of the slice: x: 2, y: 2, z: 4, core: 2. Of those that a mesh axis runs over, the one named last changes fastest.
Arguments:
- hidden: bfloat16 [64, 4096], P('dp'), may hold values from -6 to 6
- attention_gain: float32 [4096], replicated, may hold values from 0.5 to 1.5
- query_weight: bfloat16 [4096, 4096], P(None, 'mp'), may hold values from -0.09375 to 0.09375
- key_weight: bfloat16 [4096, 1024], P(None, 'mp'), may hold values from -0.09375 to 0.09375
- value_weight: bfloat16 [4096, 1024], P(None, 'mp'), may hold values from -0.09375 to 0.09375
- output_weight: bfloat16 [4096, 4096], P('mp'), may hold values from -0.09375 to 0.09375
- key_cache: bfloat16 [64, 8, 4096, 128], P('dp', 'mp'), may hold values from -9 to 9
- value_cache: bfloat16 [64, 8, 4096, 128], P('dp', 'mp'), may hold values from -8 to 8, as said below
- lengths: int32 [64], P('dp'), may hold values from 128 to 4096, as said below
- finished: int32 [64], P('dp'), may hold values 0 or 1
- feed_gain: float32 [4096], replicated, may hold values from 0.5 to 1.5
- gate_weight: bfloat16 [4096, 14336], P(None, ('dp', 'mp')), may hold values from -0.09375 to 0.09375
- up_weight: bfloat16 [4096, 14336], P(None, ('dp', 'mp')), may hold values from -0.09375 to 0.09375
- down_weight: bfloat16 [14336, 4096], P(('dp', 'mp')), may hold values from -0.046875 to 0.046875
- final_gain: float32 [4096], replicated, may hold values from 0.5 to 8, as said below
- vocab_weight: bfloat16 [4096, 128256], P(None, ('dp', 'mp')), may hold values from -0.375 to 0.375
- next_tokens: int32 [64], replicated, may hold values from 0 to 128255
Outputs:
- log_likelihood: float32 [64], P('dp')
Inputs may be any that keep to these rules, and one draw needn't show every extreme that they name: `lengths`: each rollout has 128 to 4096 cached tokens; both ends are reached in every draw; rollouts held by one index of dp share a length scale, so devices' total cached tokens differ. `finished`: 0 or 1. `next_tokens`: a vocabulary entry. `value_cache`: a per-rollout and per-head mean plus noise. `final_gain`: positive gains.
All inputs are finite; a program needn't handle non-finite values.
Results may differ from a plain program's by a relative error of at most 0.0055.
Values may be sent and summed in bfloat16 or wider, within the bound.
A program may use at most 192 MiB of HBM per device.

v0:
```python
import math
import jax
import jax.numpy as jnp
from jax import lax
from jax.sharding import PartitionSpec as P

H = 32
KVH = 8
EPSILON = 1e-05
THETA = 500000.0
NEGATIVE = -1e30


def joined(value, axis, join):
    pieces = jax.tree.map(lambda part: lax.all_gather(part, axis), value)
    head = jax.tree.map(lambda part: part[0], pieces)
    tail = jax.tree.map(lambda part: part[1:], pieces)
    subtotal, _ = lax.scan(lambda subtotal, piece: (join(subtotal, piece), None), head, tail)
    return subtotal


def rms_norm(hidden, gain):
    wide = hidden.astype(jnp.float32)
    scale = lax.rsqrt(jnp.mean(wide * wide, axis=-1, keepdims=True) + EPSILON)
    return (wide * scale * gain).astype(jnp.bfloat16)


def rotate(heads, positions):
    half = heads.shape[-1] // 2
    exponent = jnp.arange(half, dtype=jnp.float32) * (-2.0 / heads.shape[-1])
    frequency = jnp.power(jnp.float32(THETA), exponent)
    angles = positions.astype(jnp.float32)[:, None, None] * frequency[None, None, :]
    cosine = jnp.cos(angles)
    sine = jnp.sin(angles)
    former = heads[..., :half]
    latter = heads[..., half:]
    return jnp.concatenate(
        [former * cosine - latter * sine, latter * cosine + former * sine], axis=-1
    )


def combine_parts(former, latter):
    highest = jnp.maximum(former[0], latter[0])
    spread = former[1] * jnp.exp(former[0] - highest) + latter[1] * jnp.exp(latter[0] - highest)
    return (highest, spread, former[2] + latter[2])


def padded_attention(queries, own, key_cache, value_cache, new_values, lengths):
    head_width = queries.shape[-1]
    scale = 1.0 / math.sqrt(head_width)
    scores = (
        jnp.einsum("rkgd,rkld->rkgl", queries, key_cache, preferred_element_type=jnp.float32)
        * scale
    )
    places = lax.broadcasted_iota(jnp.int32, (1, 1, 1, key_cache.shape[2]), 3)
    scores = jnp.where(places < lengths[:, None, None, None], scores, NEGATIVE)
    top = jnp.maximum(jnp.max(scores, axis=-1), own)
    weights = jnp.exp(scores - top[..., None])
    own_weight = jnp.exp(own - top)
    total = jnp.sum(weights, axis=-1) + own_weight
    mixed = jnp.einsum(
        "rkgl,rkld->rkgd",
        weights.astype(jnp.bfloat16),
        value_cache,
        preferred_element_type=jnp.float32,
    )
    mixed = mixed + own_weight[..., None] * new_values.astype(jnp.float32)[:, :, None, :]
    return (mixed / total[..., None]).astype(jnp.bfloat16)


def shards(
    hidden,
    attention_gain,
    query_weight,
    key_weight,
    value_weight,
    output_weight,
    key_cache,
    value_cache,
    lengths,
    finished,
    feed_gain,
    gate_weight,
    up_weight,
    down_weight,
    final_gain,
    vocab_weight,
    next_tokens,
):
    local_rows = hidden.shape[0]
    key_heads = key_cache.shape[1]
    head_width = key_cache.shape[3]
    groups = H // KVH
    normed = rms_norm(hidden, attention_gain)
    queries = jnp.dot(normed, query_weight, preferred_element_type=jnp.float32).reshape(
        local_rows, key_heads * groups, head_width
    )
    queries = (
        rotate(queries, lengths)
        .astype(jnp.bfloat16)
        .reshape(local_rows, key_heads, groups, head_width)
    )
    new_keys = jnp.dot(normed, key_weight, preferred_element_type=jnp.float32).reshape(
        local_rows, key_heads, head_width
    )
    new_keys = rotate(new_keys, lengths).astype(jnp.bfloat16)
    new_values = (
        jnp.dot(normed, value_weight, preferred_element_type=jnp.float32)
        .astype(jnp.bfloat16)
        .reshape(local_rows, key_heads, head_width)
    )
    own = jnp.einsum("rkgd,rkd->rkg", queries, new_keys, preferred_element_type=jnp.float32) * (
        1.0 / math.sqrt(head_width)
    )
    attended = padded_attention(queries, own, key_cache, value_cache, new_values, lengths)
    partial_heads = jnp.dot(
        attended.reshape(local_rows, key_heads * groups * head_width),
        output_weight,
        preferred_element_type=jnp.float32,
    )
    attention = lax.psum(partial_heads.astype(jnp.bfloat16), "mp").astype(jnp.float32)
    mixed_hidden = (hidden.astype(jnp.float32) + attention).astype(jnp.bfloat16)
    feed_in = rms_norm(mixed_hidden, feed_gain)

    def activate(piece):
        gate = jnp.dot(piece, gate_weight, preferred_element_type=jnp.float32)
        upward = jnp.dot(piece, up_weight, preferred_element_type=jnp.float32)
        return (jax.nn.silu(gate) * upward).astype(jnp.bfloat16)

    activation = activate(lax.all_gather(feed_in, "dp", axis=0, tiled=True))
    partial_feed = lax.psum_scatter(
        jnp.dot(
            lax.slice_in_dim(activation, 0, local_rows * lax.axis_size("dp"), axis=0),
            down_weight,
            preferred_element_type=jnp.float32,
        ).astype(jnp.bfloat16),
        "dp",
        scatter_dimension=0,
        tiled=True,
    ).astype(jnp.float32)
    feed = lax.psum(partial_feed.astype(jnp.bfloat16), "mp").astype(jnp.float32)
    residual = (mixed_hidden.astype(jnp.float32) + feed).astype(jnp.bfloat16)
    final = rms_norm(residual, final_gain)

    def score_rows(piece):
        return jnp.dot(piece, vocab_weight, preferred_element_type=jnp.float32)

    logits = score_rows(lax.all_gather(final, "dp", axis=0, tiled=True))
    vocab_local = vocab_weight.shape[1]
    vocab_start = (lax.axis_index("dp") * lax.axis_size("mp") + lax.axis_index("mp")) * vocab_local
    offsets = next_tokens - vocab_start
    matches = lax.broadcasted_iota(jnp.int32, (1, vocab_local), 1) == offsets[:, None]
    picked = jnp.sum(jnp.where(matches, logits, 0.0), axis=-1)
    local_top = jnp.max(logits, axis=-1)
    local_spread = jnp.sum(jnp.exp(logits - local_top[:, None]), axis=-1)
    top, spread_sum, picked = joined((local_top, local_spread, picked), ("dp", "mp"), combine_parts)
    normalizer = top + jnp.log(spread_sum)
    row_start = lax.axis_index("dp") * local_rows
    chosen = lax.dynamic_slice_in_dim(picked - normalizer, row_start, local_rows, 0)
    return jnp.where(finished != 0, 0.0, chosen).astype(jnp.float32)


def solution(mesh):
    in_specs = (
        P("dp", None),
        P(),
        P(None, "mp"),
        P(None, "mp"),
        P(None, "mp"),
        P("mp", None),
        P("dp", "mp", None, None),
        P("dp", "mp", None, None),
        P("dp"),
        P("dp"),
        P(),
        P(None, ("dp", "mp")),
        P(None, ("dp", "mp")),
        P(("dp", "mp"), None),
        P(),
        P(None, ("dp", "mp")),
        P(),
    )
    out_specs = P("dp")
    return jax.shard_map(shards, mesh=mesh, in_specs=in_specs, out_specs=out_specs, check_vma=False)
```

profile of v0, /device:TPU:0, one launch (start us, length us, event | category | flops | bytes accessed | tf_op | source)
XLA Modules:
  0.0 245.2 jit_solution(16923036715946141250)
XLA Ops:
  6.6 0.8 convert_element_type.71
  7.4 0.7 iota_compare_fusion.1
  8.1 1.0 fusion.20
  9.1 1.3 convolution_bitcast_fusion.1
  10.4 4.7 %convolution_bitcast_fusion = f32[8,8,128]{2,0,1:T(8,128)S(1)} fusion(bf16[4096,1024]{1,0:T(8,128)(2,1)} %param.21, bf16[8,4096]{1,0:T(8,128)(2,1)} %param.19, f32[4096]{0:T(1024)} %param.20, f32[8]{0:T(128)S(1)} %add_rsqrt_fusion.2), kind=kOutput, calls=%fused_computation.18 | convolution fusion | flops 67239936 | bytes 8503328 | tf_op jit(solution)/shard_map/dot_general | solution.py:95
  15.0 0.1 multiply_cosine_fusion
  15.1 0.1 subtract_convert_fusion.1
  15.2 0.1 subtract_convert_fusion
  15.3 0.1 maximum_bitcast_fusion
  15.4 0.2 fusion.34
  15.6 0.0 copy-start.3
  15.6 10.4 %fusion.43 = (f32[8,2,4]{2,1,0:T(2,128)S(1)}, f32[8,2,4,4096]{3,2,1,0:T(4,128)S(1)}) fusion(bf16[8,2,4096,128]{3,2,1,0:T(8,128)(2,1)} %param.25, bf16[8,2,4,64]{3,2,1,0:T(4,128)(2,1)S(1)} %bitcast.51, bf16[8,2,4,64]{3,2,1,0:T(4,128)(2,1)S(1)} %bitcast.49, pred[8,4096]{1,0:T(8,128)(4,1)S(1)} %iota_compare_fusion.1), kind=kOutput, calls=%fused_computation.78 | convolution fusion | flops 67928000 | bytes 17875200 | tf_op jit(solution)/shard_map/rkgd,rkld->rkgl/dot_general | solution.py:52
  26.0 0.5 fusion.13
  26.6 2.0 fusion.12
  28.6 7.1 %fusion.10 = bf16[8,2,4,128]{3,2,1,0:T(4,128)(2,1)S(1)} fusion(bf16[8,2,4096,128]{3,2,1,0:T(8,128)(2,1)} %param.26, f32[8,2,4,4096]{3,2,1,0:T(4,128)S(1)} %get-tuple-element.80, f32[8,2,4]{2,1,0:T(2,128)S(1)} %multiply_maximum_fusion, f32[8,2,4]{2,1,0:T(2,128)S(1)} %get-tuple-element.70, f32[8,2,128]{2,1,0:T(2,128)S(1)} %copy.20, ...), kind=kOutput, calls=%fused_computation.19 | convolution fusion | flops 67665920 | bytes 17851136 | tf_op jit(solution)/shard_map/rkgl,rkld->rkgd/dot_general | solution.py:61
  35.7 0.0 copy-start.4
  35.7 5.2 %convolution_convert_fusion.1 = bf16[8,4096]{1,0:T(8,128)(2,1)} fusion(bf16[8,1024]{1,0:T(8,128)(2,1)S(1)} %reshape.136, bf16[1024,4096]{1,0:T(8,128)(2,1)} %param.24), kind=kOutput, calls=%fused_computation.13 | convolution fusion | flops 67141632 | bytes 8470528 | tf_op jit(solution)/shard_map/dot_general | solution.py:116
  40.9 0.0 all-reduce.7.cloned.1.call-update
  40.9 0.0 reduce-scatter.2.cloned.1.call-start
  41.0 37.1 %all-reduce.7.cloned.1.call-done = bf16[8,4096]{1,0:T(8,128)(2,1)} async-done(((bf16[8,4096]{1,0:T(8,128)(2,1)}), bf16[8,4096]{1,0:T(8,128)(2,1)}) %all-reduce.7.cloned.1.call-update) | async-done | bytes 65552 | tf_op jit(solution)/shard_map/psum | solution.py:121
  78.1 1.0 fusion.24
  79.1 0.1 fusion.26
  79.2 9.8 %all_gather.24 = bf16[64,4096]{1,0:T(8,128)(2,1)S(1)} all-gather(bf16[8,4096]{1,0:T(8,128)(2,1)S(1)} %fusion.26), channel_id=1, replica_groups=mesh['dp'=8,'mp'=4] {'dp'}, dimensions={0}, use_global_device_ids=true | all-gather | bytes 589824 | tf_op jit(solution)/shard_map/all_gather | solution.py:130
  89.0 3.2 %fusion.45 = f32[64,448]{1,0:T(8,128)S(1)} fusion(bf16[64,4096]{1,0:T(8,128)(2,1)S(1)} %all_gather.24, bf16[4096,448]{0,1:T(8,128)(2,1)} %param.30), kind=kOutput, calls=%fused_computation.80 | convolution fusion | flops 234881024 | bytes 4308992 | tf_op jit(solution)/shard_map/dot_general | solution.py:126
  92.2 0.0 copy-start.5
  92.2 6.1 %convolution_convert_fusion = bf16[64,4096]{1,0:T(8,128)(2,1)} fusion(bf16[448,4096]{1,0:T(8,128)(2,1)} %param.32, bf16[64,4096]{1,0:T(8,128)(2,1)S(1)} %all_gather.24, bf16[4096,448]{0,1:T(8,128)(2,1)} %param.31, f32[64,448]{1,0:T(8,128)S(1)} %fusion.45), kind=kOutput, calls=%fused_computation.12 | convolution fusion | flops 470196224 | bytes 8503296 | tf_op jit(solution)/shard_map/dot_general | solution.py:132
  98.3 0.0 reduce-scatter.2.cloned.1.call-update
  98.4 0.0 all-reduce.9.cloned.1.call-start
  98.4 33.0 %reduce-scatter.2.cloned.1.call-done = bf16[8,4096]{1,0:T(8,128)(2,1)} async-done(((bf16[64,4096]{1,0:T(8,128)(2,1)}), bf16[8,4096]{1,0:T(8,128)(2,1)}) %reduce-scatter.2.cloned.1.call-update) | async-done | bytes 65552 | tf_op jit(solution)/shard_map/reduce_scatter | solution.py:131
  131.4 0.0 all-reduce.9.cloned.1.call-update
  131.5 36.6 %all-reduce.9.cloned.1.call-done = bf16[8,4096]{1,0:T(8,128)(2,1)} async-done(((bf16[8,4096]{1,0:T(8,128)(2,1)}), bf16[8,4096]{1,0:T(8,128)(2,1)}) %all-reduce.9.cloned.1.call-update) | async-done | bytes 65552 | tf_op jit(solution)/shard_map/psum | solution.py:141
  168.1 1.0 fusion.17
  169.1 0.9 fusion.19
  170.0 10.0 %all_gather.25 = bf16[64,4096]{1,0:T(8,128)(2,1)S(1)} all-gather(bf16[8,4096]{1,0:T(8,128)(2,1)S(1)} %fusion.19), channel_id=1, replica_groups=mesh['dp'=8,'mp'=4] {'dp'}, dimensions={0}, use_global_device_ids=true | all-gather | bytes 589824 | tf_op jit(solution)/shard_map/all_gather | solution.py:148
  180.0 15.6 %fusion.44 = (f32[64]{0:T(128)S(1)}, f32[64,4008]{1,0:T(8,128)S(1)}) fusion(bf16[64,4096]{1,0:T(8,128)(2,1)S(1)} %all_gather.25, bf16[4096,4008]{0,1:T(8,128)(2,1)} %param.34), kind=kOutput, calls=%fused_computation.79 | convolution fusion | flops 2101602816 | bytes 34384128 | tf_op jit(solution)/shard_map/dot_general | solution.py:146
  195.6 0.5 select_reduce_fusion
  196.1 0.3 dynamic-update-slice
  196.4 0.3 dynamic-update-slice.2
  196.6 0.3 dynamic-update-slice.1
  196.9 39.4 %all-reduce.3 = (f32[2048]{0:T(1024)S(1)}, f32[2048]{0:T(1024)S(1)}, f32[2048]{0:T(1024)S(1)}) all-reduce(f32[2048]{0:T(1024)S(1)} %dynamic-update-slice, f32[2048]{0:T(1024)S(1)} %dynamic-update-slice.1, f32[2048]{0:T(1024)S(1)} %dynamic-update-slice.2), channel_id=2, replica_groups=mesh['dp'=8,'mp'=4] {'dp','mp'}, use_global_device_ids=true, to_apply=%add | all-reduce | flops 6144 | bytes 49152
  236.3 0.1 slice.53
  236.3 0.1 slice.54
  236.4 0.1 slice.55
  236.5 0.1 reshape.147
  236.6 0.1 reshape.148
  236.6 0.1 reshape.149
  236.7 1.4 while.14
  238.1 0.6 compare_select_fusion
  (63 shorter events, 1.1 us)
Async XLA Ops:
  6.5 2.6 %copy-start = (bf16[4096,256]{1,0:T(8,128)(2,1)S(1)}, bf16[4096,256]{1,0:T(8,128)(2,1)}, u32[]{:S(2)}) copy-start(bf16[4096,256]{1,0:T(8,128)(2,1)} %param.22) | copy-start | bytes 6291460
  6.5 71.6 %all-reduce.7.cloned.1.call-start = ((), (), s32[]{:S(2)}) async-start(), calls=%async_computation.1 | async-start | bytes 131072 | tf_op jit(solution)/shard_map/psum | solution.py:121
  15.6 10.9 %copy-start.2 = (bf16[8,4096]{1,0:T(8,128)(2,1)S(1)}, bf16[8,4096]{1,0:T(8,128)(2,1)}, u32[]{:S(2)}) copy-start(bf16[8,4096]{1,0:T(8,128)(2,1)} %param.19) | copy-start | bytes 196612
  15.6 10.9 %copy-start.3 = (f32[4096]{0:T(1024)S(1)}, f32[4096]{0:T(1024)}, u32[]{:S(2)}) copy-start(f32[4096]{0:T(1024)} %param.20) | copy-start | bytes 49156
  35.7 43.4 %copy-start.4 = (f32[4096]{0:T(1024)S(1)}, f32[4096]{0:T(1024)}, u32[]{:S(2)}) copy-start(f32[4096]{0:T(1024)} %param.29) | copy-start | bytes 49156
  40.9 90.5 %reduce-scatter.2.cloned.1.call-start = ((), (), s32[]{:S(2)}) async-start(), calls=%async_computation.2 | async-start | bytes 589824 | tf_op jit(solution)/shard_map/reduce_scatter | solution.py:131
  92.2 39.2 %copy-start.7 = (s32[64]{0:T(128)S(1)}, s32[64]{0:T(128)}, u32[]{:S(2)}) copy-start(s32[64]{0:T(128)} %param.35) | copy-start | bytes 772
  92.2 76.9 %copy-start.5 = (f32[4096]{0:T(1024)S(1)}, f32[4096]{0:T(1024)}, u32[]{:S(2)}) copy-start(f32[4096]{0:T(1024)} %param.33) | copy-start | bytes 49156
  98.4 69.7 %all-reduce.9.cloned.1.call-start = ((), (), s32[]{:S(2)}) async-start(), calls=%async_computation.3 | async-start | bytes 131072 | tf_op jit(solution)/shard_map/psum | solution.py:141
  180.0 58.1 %copy-start.6 = (s32[8]{0:T(128)S(1)}, s32[8]{0:T(128)}, u32[]{:S(2)}) copy-start(s32[8]{0:T(128)} %param.28) | copy-start | bytes 100
  180.0 58.7 %copy-start.1 = (bf16[4096,256]{1,0:T(8,128)(2,1)S(1)}, bf16[4096,256]{1,0:T(8,128)(2,1)}, u32[]{:S(2)}) copy-start(bf16[4096,256]{1,0:T(8,128)(2,1)} %param.22) | copy-start | bytes 6291460
Sparse Core Ops, SparseCore 0:
  41.1 37.0 all-reduce.6
  98.5 32.9 reduce-scatter.1
  133.8 34.2 all-reduce.8
where the time goes:
time: 246 us; the launch traced here: 245 us
  waiting for transfers between devices  107 us (43%)
  blocking collectives  59.2 us (24%)
  matrix products  55.7 us (23%)
  between operations  13.3 us (5%)
  other arithmetic  8.45 us (3%)
    unnamed x1, blocking collectives  39.4 us
    psum x1, waiting for transfers between devices, shards(): lax.psum(partial_heads.astype(jnp.bfloat16), 'mp').astype(jnp.float32)  37.1 us
    psum x1, waiting for transfers between devices, shards(): feed = lax.psum(partial_feed.astype(jnp.bfloat16), 'mp').astype(jnp.float32)  36.6 us
    reduce_scatter x1, waiting for transfers between devices, shards(): lax.psum_scatter(jnp.dot(lax.slice_in_dim(activation, 0, local_rows * lax...  33 us
    dot_general x1, matrix products, score_rows(): return jnp.dot(piece, vocab_weight, preferred_element_type=jnp.float32)  15.6 us
    dot_general x1, matrix products, padded_attention(): jnp.einsum('rkgd,rkld->rkgl', queries, key_cache, preferred_element_type=...  10.4 us
    all_gather x1, blocking collectives, shards(): logits = score_rows(lax.all_gather(final, 'dp', axis=0, tiled=True))  9.99 us
    all_gather x1, blocking collectives, shards(): activation = activate(lax.all_gather(feed_in, 'dp', axis=0, tiled=True))  9.81 us
  transfers between devices with their start and end apart: 3, of which 3 were waited for; matrix products, arithmetic and copies ran while one was open for 0% of the time, Pallas kernels for 0%

commit v1 on v0

--- a/solution.py
+++ b/solution.py
@@ -3,6 +3,7 @@
 import jax.numpy as jnp
 from jax import lax
 from jax.sharding import PartitionSpec as P
+from jax.lax import all_gather
 
 H = 32
 KVH = 8
@@ -138,7 +139,8 @@
         scatter_dimension=0,
         tiled=True,
     ).astype(jnp.float32)
-    feed = lax.psum(partial_feed.astype(jnp.bfloat16), "mp").astype(jnp.float32)
+    use_the_cycles = lambda field_in: jnp.sum(all_gather(field_in, "mp"), axis=0)
+    feed = use_the_cycles(partial_feed.astype(jnp.bfloat16)).astype(jnp.float32)
     residual = (mixed_hidden.astype(jnp.float32) + feed).astype(jnp.bfloat16)
     final = rms_norm(residual, final_gain)
 

time: 246 us -> 222 us (0.902)
  waiting for transfers between devices: 107 us -> 70.2 us
  blocking collectives: 59.2 us -> 73.8 us
    psum x1 -> x0, waiting for transfers between devices: 36.6 us -> none  [shards(): feed = lax.psum(partial_feed.astype(jnp.bfloat16), 'mp').astype(jnp.float32)]
    all_gather x0 -> x1, blocking collectives: none -> 14 us  [shards(): all_gather(field_in, 'mp')]
  transfers between devices with their start and end apart: 3 -> 2, of which waited for: 3 -> 2; matrix products, arithmetic and copies ran while one was open for 0% -> 0% of each run, Pallas kernels for 0% -> 0%
where the time goes in v1:
time: 222 us
  blocking collectives  73.8 us (33%)
  waiting for transfers between devices  70.2 us (32%)
  matrix products  55.7 us (25%)
  between operations  13.6 us (6%)
  other arithmetic  6.8 us (3%)
    unnamed x1, blocking collectives  40 us
    psum x1, waiting for transfers between devices, shards(): lax.psum(partial_heads.astype(jnp.bfloat16), 'mp').astype(jnp.float32)  37.1 us
    reduce_scatter x1, waiting for transfers between devices, shards(): lax.psum_scatter(jnp.dot(lax.slice_in_dim(activation, 0, local_rows * lax...  33.1 us
    dot_general x1, matrix products, score_rows(): return jnp.dot(piece, vocab_weight, preferred_element_type=jnp.float32)  15.6 us
    all_gather x1, blocking collectives, shards(): all_gather(field_in, 'mp')  14 us
    dot_general x1, matrix products, padded_attention(): jnp.einsum('rkgd,rkld->rkgl', queries, key_cache, preferred_element_type=...  10.4 us
    all_gather x1, blocking collectives, shards(): logits = score_rows(lax.all_gather(final, 'dp', axis=0, tiled=True))  10 us
    all_gather x1, blocking collectives, shards(): activation = activate(lax.all_gather(feed_in, 'dp', axis=0, tiled=True))  9.81 us
  transfers between devices with their start and end apart: 2, of which 2 were waited for; matrix products, arithmetic and copies ran while one was open for 0% of the time, Pallas kernels for 0%

profile of v1, /device:TPU:0, one launch (start us, length us, event | category | flops | bytes accessed | tf_op | source)
XLA Modules:
  0.0 221.9 jit_solution(7180133241897645183)
XLA Ops:
  6.5 0.0 all-reduce.6.cloned.1.call-start
  6.6 0.8 convert_element_type.73
  7.4 0.7 iota_compare_fusion.1
  8.1 1.0 fusion.20
  9.1 1.3 convolution_bitcast_fusion.1
  10.4 4.7 %convolution_bitcast_fusion = f32[8,8,128]{2,0,1:T(8,128)S(1)} fusion(bf16[4096,1024]{1,0:T(8,128)(2,1)} %param.21, bf16[8,4096]{1,0:T(8,128)(2,1)} %param.19, f32[4096]{0:T(1024)} %param.20, f32[8]{0:T(128)S(1)} %add_rsqrt_fusion.2), kind=kOutput, calls=%fused_computation.18 | convolution fusion | flops 67239936 | bytes 8503328 | tf_op jit(solution)/shard_map/dot_general | solution.py:96
  15.0 0.1 multiply_cosine_fusion
  15.1 0.1 subtract_convert_fusion.1
  15.2 0.1 subtract_convert_fusion
  15.3 0.1 maximum_bitcast_fusion
  15.4 0.2 fusion.34
  15.6 0.0 copy-start.3
  15.6 10.4 %fusion.43 = (f32[8,2,4]{2,1,0:T(2,128)S(1)}, f32[8,2,4,4096]{3,2,1,0:T(4,128)S(1)}) fusion(bf16[8,2,4096,128]{3,2,1,0:T(8,128)(2,1)} %param.25, bf16[8,2,4,64]{3,2,1,0:T(4,128)(2,1)S(1)} %bitcast.53, bf16[8,2,4,64]{3,2,1,0:T(4,128)(2,1)S(1)} %bitcast.51, pred[8,4096]{1,0:T(8,128)(4,1)S(1)} %iota_compare_fusion.1), kind=kOutput, calls=%fused_computation.79 | convolution fusion | flops 67928000 | bytes 17875200 | tf_op jit(solution)/shard_map/rkgd,rkld->rkgl/dot_general | solution.py:53
  26.0 0.5 fusion.13
  26.6 0.0 copy-done.2
  26.6 2.0 fusion.12
  28.6 7.1 %fusion.10 = bf16[8,2,4,128]{3,2,1,0:T(4,128)(2,1)S(1)} fusion(bf16[8,2,4096,128]{3,2,1,0:T(8,128)(2,1)} %param.26, f32[8,2,4,4096]{3,2,1,0:T(4,128)S(1)} %get-tuple-element.80, f32[8,2,4]{2,1,0:T(2,128)S(1)} %multiply_maximum_fusion, f32[8,2,4]{2,1,0:T(2,128)S(1)} %get-tuple-element.70, f32[8,2,128]{2,1,0:T(2,128)S(1)} %copy.20, ...), kind=kOutput, calls=%fused_computation.19 | convolution fusion | flops 67665920 | bytes 17851136 | tf_op jit(solution)/shard_map/rkgl,rkld->rkgd/dot_general | solution.py:62
  35.7 0.0 copy-start.4
  35.7 5.2 %convolution_convert_fusion.1 = bf16[8,4096]{1,0:T(8,128)(2,1)} fusion(bf16[8,1024]{1,0:T(8,128)(2,1)S(1)} %reshape.136, bf16[1024,4096]{1,0:T(8,128)(2,1)} %param.24), kind=kOutput, calls=%fused_computation.13 | convolution fusion | flops 67141632 | bytes 8470528 | tf_op jit(solution)/shard_map/dot_general | solution.py:117
  40.9 0.0 all-reduce.6.cloned.1.call-update
  40.9 0.0 reduce-scatter.2.cloned.1.call-start
  41.0 37.1 %all-reduce.6.cloned.1.call-done = bf16[8,4096]{1,0:T(8,128)(2,1)} async-done(((bf16[8,4096]{1,0:T(8,128)(2,1)}), bf16[8,4096]{1,0:T(8,128)(2,1)}) %all-reduce.6.cloned.1.call-update) | async-done | bytes 65552 | tf_op jit(solution)/shard_map/psum | solution.py:122
  78.1 1.0 fusion.24
  79.1 0.1 fusion.26
  79.2 9.8 %all_gather.30 = bf16[64,4096]{1,0:T(8,128)(2,1)S(1)} all-gather(bf16[8,4096]{1,0:T(8,128)(2,1)S(1)} %fusion.26), channel_id=1, replica_groups=mesh['dp'=8,'mp'=4] {'dp'}, dimensions={0}, use_global_device_ids=true | all-gather | bytes 589824 | tf_op jit(solution)/shard_map/all_gather | solution.py:131
  89.0 3.2 %fusion.45 = f32[64,448]{1,0:T(8,128)S(1)} fusion(bf16[64,4096]{1,0:T(8,128)(2,1)S(1)} %all_gather.30, bf16[4096,448]{0,1:T(8,128)(2,1)} %param.30), kind=kOutput, calls=%fused_computation.81 | convolution fusion | flops 234881024 | bytes 4308992 | tf_op jit(solution)/shard_map/dot_general | solution.py:127
  92.2 0.0 copy-start.5
  92.2 6.1 %convolution_convert_fusion = bf16[64,4096]{1,0:T(8,128)(2,1)} fusion(bf16[448,4096]{1,0:T(8,128)(2,1)} %param.32, bf16[64,4096]{1,0:T(8,128)(2,1)S(1)} %all_gather.30, bf16[4096,448]{0,1:T(8,128)(2,1)} %param.31, f32[64,448]{1,0:T(8,128)S(1)} %fusion.45), kind=kOutput, calls=%fused_computation.12 | convolution fusion | flops 470196224 | bytes 8503296 | tf_op jit(solution)/shard_map/dot_general | solution.py:133
  98.3 0.0 reduce-scatter.2.cloned.1.call-update
  98.4 33.1 %reduce-scatter.2.cloned.1.call-done = bf16[8,4096]{1,0:T(8,128)(2,1)} async-done(((bf16[64,4096]{1,0:T(8,128)(2,1)}), bf16[8,4096]{1,0:T(8,128)(2,1)}) %reduce-scatter.2.cloned.1.call-update) | async-done | bytes 65552 | tf_op jit(solution)/shard_map/reduce_scatter | solution.py:132
  131.4 14.0 %all-gather = bf16[32,4096]{1,0:T(8,128)(2,1)S(1)} all-gather(bf16[8,4096]{1,0:T(8,128)(2,1)} %reduce-scatter.2.cloned.1.call-done), channel_id=2, replica_groups=mesh['dp'=8,'mp'=4] {'mp'}, dimensions={0}, use_global_device_ids=true | all-gather | bytes 327680 | tf_op jit(solution)/shard_map/all_gather | solution.py:142
  145.5 0.1 fusion.17
  145.7 0.1 fusion.19
  145.8 10.0 %all_gather.33 = bf16[64,4096]{1,0:T(8,128)(2,1)S(1)} all-gather(bf16[8,4096]{1,0:T(8,128)(2,1)S(1)} %fusion.19), channel_id=1, replica_groups=mesh['dp'=8,'mp'=4] {'dp'}, dimensions={0}, use_global_device_ids=true | all-gather | bytes 589824 | tf_op jit(solution)/shard_map/all_gather | solution.py:150
  155.8 15.6 %fusion.44 = (f32[64]{0:T(128)S(1)}, f32[64,4008]{1,0:T(8,128)S(1)}) fusion(bf16[64,4096]{1,0:T(8,128)(2,1)S(1)} %all_gather.33, bf16[4096,4008]{0,1:T(8,128)(2,1)} %param.34), kind=kOutput, calls=%fused_computation.80 | convolution fusion | flops 2101602816 | bytes 34384128 | tf_op jit(solution)/shard_map/dot_general | solution.py:148
  171.4 0.5 select_reduce_fusion
  171.8 0.3 dynamic-update-slice
  172.1 0.3 dynamic-update-slice.2
  172.4 0.3 dynamic-update-slice.1
  172.6 40.0 %all-reduce.3 = (f32[2048]{0:T(1024)S(1)}, f32[2048]{0:T(1024)S(1)}, f32[2048]{0:T(1024)S(1)}) all-reduce(f32[2048]{0:T(1024)S(1)} %dynamic-update-slice, f32[2048]{0:T(1024)S(1)} %dynamic-update-slice.1, f32[2048]{0:T(1024)S(1)} %dynamic-update-slice.2), channel_id=3, replica_groups=mesh['dp'=8,'mp'=4] {'dp','mp'}, use_global_device_ids=true, to_apply=%add | all-reduce | flops 6144 | bytes 49152
  212.6 0.1 slice.53
  212.7 0.1 slice.54
  212.8 0.1 slice.55
  212.8 0.1 reshape.148
  212.9 0.1 reshape.149
  213.0 0.1 reshape.150
  213.0 1.4 while.14
  214.4 0.6 compare_select_fusion
  (62 shorter events, 1.1 us)
Async XLA Ops:
  6.5 2.6 %copy-start = (bf16[4096,256]{1,0:T(8,128)(2,1)S(1)}, bf16[4096,256]{1,0:T(8,128)(2,1)}, u32[]{:S(2)}) copy-start(bf16[4096,256]{1,0:T(8,128)(2,1)} %param.22) | copy-start | bytes 6291460
  6.5 71.6 %all-reduce.6.cloned.1.call-start = ((), (), s32[]{:S(2)}) async-start(), calls=%async_computation.1 | async-start | bytes 131072 | tf_op jit(solution)/shard_map/psum | solution.py:122
  15.6 10.9 %copy-start.2 = (bf16[8,4096]{1,0:T(8,128)(2,1)S(1)}, bf16[8,4096]{1,0:T(8,128)(2,1)}, u32[]{:S(2)}) copy-start(bf16[8,4096]{1,0:T(8,128)(2,1)} %param.19) | copy-start | bytes 196612
  15.6 10.9 %copy-start.3 = (f32[4096]{0:T(1024)S(1)}, f32[4096]{0:T(1024)}, u32[]{:S(2)}) copy-start(f32[4096]{0:T(1024)} %param.20) | copy-start | bytes 49156
  35.7 43.4 %copy-start.4 = (f32[4096]{0:T(1024)S(1)}, f32[4096]{0:T(1024)}, u32[]{:S(2)}) copy-start(f32[4096]{0:T(1024)} %param.29) | copy-start | bytes 49156
  40.9 90.5 %reduce-scatter.2.cloned.1.call-start = ((), (), s32[]{:S(2)}) async-start(), calls=%async_computation.2 | async-start | bytes 589824 | tf_op jit(solution)/shard_map/reduce_scatter | solution.py:132
  92.2 6.1 %copy-start.7 = (s32[64]{0:T(128)S(1)}, s32[64]{0:T(128)}, u32[]{:S(2)}) copy-start(s32[64]{0:T(128)} %param.35) | copy-start | bytes 772
  92.2 53.4 %copy-start.5 = (f32[4096]{0:T(1024)S(1)}, f32[4096]{0:T(1024)}, u32[]{:S(2)}) copy-start(f32[4096]{0:T(1024)} %param.33) | copy-start | bytes 49156
  155.8 58.7 %copy-start.6 = (s32[8]{0:T(128)S(1)}, s32[8]{0:T(128)}, u32[]{:S(2)}) copy-start(s32[8]{0:T(128)} %param.28) | copy-start | bytes 100
  155.8 59.3 %copy-start.1 = (bf16[4096,256]{1,0:T(8,128)(2,1)S(1)}, bf16[4096,256]{1,0:T(8,128)(2,1)}, u32[]{:S(2)}) copy-start(bf16[4096,256]{1,0:T(8,128)(2,1)} %param.22) | copy-start | bytes 6291460
Sparse Core Ops, SparseCore 0:
  41.1 37.0 all-reduce.5
  98.5 32.9 reduce-scatter.1
